TPU v7x, 128 devices: a whole 4x4x4 slice. The times are simulated.
128 devices in a mesh: samp: 16 (over z, x), feat: 8 (over y, core).
Axes of the slice: x: 4, y: 4, z: 4, core: 2. Of those that a mesh axis runs over, the one named last changes fastest.
Arguments:
- features: bfloat16 [262144, 2048], P('samp', 'feat'), may hold values from -40 to 40
- labels: int32 [262144], P('samp'), may hold values from 0 to 9
- weights: float32 [10, 2048], P(None, 'feat'), may hold values from -6 to 6
- sketch_basis: float32 [10, 2048, 512], P(None, 'feat'), may hold values from -0.0390625 to 0.0390625
- sketch_values: float32 [512], replicated, may hold values from 0.05 to 2
Outputs:
- newton_step: float32 [10, 2048], P(None, 'feat')
All inputs are finite; a program needn't handle non-finite values.
Results may differ from a plain program's by a relative error of at most 0.001.
The roundings to bfloat16 on the way count: a program that leaves them out, or rounds other values in their place, can miss the bound.
Values may be sent and summed in bfloat16 or wider, within the bound.
A program may use at most 128 MiB of HBM per device.

v0:
```python
import math
import jax
import jax.numpy as jnp
from jax import lax
from jax.sharding import PartitionSpec as P

F = 2048
ITERS = 3
ridge = 0.05
contract_last = (((1,), (1,)), ((), ()))
contract_first = (((0,), (0,)), ((), ()))


def copy_for_each(shard, axis):
    devices = lax.axis_size(axis)
    return lax.all_to_all(
        jnp.broadcast_to(shard[None], (devices, *shard.shape)), axis, 0, 0, tiled=True
    )


def of_everyone(shard, axis):
    everything = copy_for_each(shard, axis)
    return jnp.sum(everything, axis=0)


def in_blocks(shard, dim, devices):
    before, after = (shard.shape[:dim], shard.shape[dim + 1 :])
    return jnp.moveaxis(shard.reshape(*before, devices, -1, *after), dim, 0)


def summed_on_arrival(shard, axis, dim):
    devices = lax.axis_size(axis)
    pieces = lax.all_to_all(in_blocks(shard, dim, devices), axis, 0, 0, tiled=True)
    return jnp.sum(pieces, axis=0)


def column_softmax(scores):
    column_max = jnp.max(scores, axis=0, keepdims=True)
    shifted_exp = jnp.exp(scores - column_max)
    return shifted_exp / jnp.sum(shifted_exp, axis=0, keepdims=True)


def total_one(amount):
    return of_everyone(amount, "feat")


def on_device(features, labels, weights, sketch_basis, sketch_values):
    classes, local_cols = weights.shape
    local_rows = features.shape[0]
    sketch_rank = sketch_basis.shape[2]
    samp_count = lax.axis_size("samp")
    feat_count = lax.axis_size("feat")
    total_rows = local_rows * samp_count
    row_features = lax.all_to_all(features, "feat", split_axis=0, concat_axis=1, tiled=True)
    share_rows = local_rows // feat_count
    row_start = lax.axis_index("feat") * share_rows
    own_labels = lax.dynamic_slice_in_dim(labels, row_start, share_rows, 0)
    onehot = (own_labels[None, :] == jnp.arange(classes, dtype=jnp.int32)[:, None]).astype(
        jnp.float32
    )

    def class_logits(rounded):
        partial_logits = lax.dot_general(
            rounded, row_features, contract_last, preferred_element_type=jnp.float32
        )
        return partial_logits

    def feature_sums(coeffs):
        coeffs_b = coeffs.astype(jnp.bfloat16)
        whole_cols = jnp.dot(coeffs_b, row_features, preferred_element_type=jnp.float32)
        partial_cols = summed_on_arrival(whole_cols, "feat", 1)
        return of_everyone(partial_cols, "samp")

    weights_b = weights.astype(jnp.bfloat16)
    weights_b = lax.all_gather(weights_b, "feat", axis=1, tiled=True)
    probabilities = column_softmax(class_logits(weights_b) / math.sqrt(F))
    gradient = feature_sums(probabilities - onehot) * (math.sqrt(F) / total_rows) + ridge * weights
    flat_local = sketch_basis.reshape(classes * local_cols, sketch_rank)
    local_gram = lax.dot_general(
        flat_local, flat_local, contract_first, precision=lax.Precision.HIGHEST
    )
    gram_matrix = lax.psum(local_gram, "feat")
    factor = jnp.linalg.cholesky(gram_matrix)
    coefficients = (jnp.min(sketch_values) + ridge) / (sketch_values + ridge) - 1.0
    basis_own = sketch_basis.reshape(classes * local_cols, sketch_rank)

    def precondition(residue):
        local_proj = jnp.dot(residue.reshape(-1), basis_own, precision=lax.Precision.HIGHEST)
        projection = total_one(local_proj)
        inner_coords = jax.scipy.linalg.solve_triangular(factor, projection, lower=True)
        weighted_coords = coefficients * inner_coords
        outer_coords = jax.scipy.linalg.solve_triangular(
            factor, weighted_coords, lower=True, trans=1
        )
        scaled_res = residue + jnp.dot(
            basis_own, outer_coords, precision=lax.Precision.HIGHEST
        ).reshape(residue.shape)
        return (scaled_res, total_one(jnp.sum(residue * scaled_res)))

    residue = -gradient
    newton_part = jnp.zeros_like(residue)
    scaled_res, res_dot = precondition(residue)
    direction = scaled_res
    for iteration in range(ITERS):
        hessian_rounded = direction.astype(jnp.bfloat16)
        gathered = hessian_rounded
        gathered = lax.all_gather(gathered, "feat", axis=1, tiled=True)
        image_vals = class_logits(gathered)
        weighted = probabilities * image_vals
        curvature = weighted - probabilities * jnp.sum(weighted, axis=0, keepdims=True)
        hess_image = feature_sums(curvature) / total_rows + ridge * direction
        step_size = res_dot / total_one(jnp.sum(direction * hess_image))
        newton_part = newton_part + step_size * direction
        if iteration + 1 < ITERS:
            residue = residue - step_size * hess_image
            scaled_res, new_dot = precondition(residue)
            direction = scaled_res + new_dot / res_dot * direction
            res_dot = new_dot
    return newton_part


def solution(mesh):
    in_specs = (P("samp", "feat"), P("samp"), P(None, "feat"), P(None, "feat", None), P())
    out_specs = P(None, "feat")
    return jax.shard_map(
        on_device, mesh=mesh, in_specs=in_specs, out_specs=out_specs, check_vma=False
    )
```

profile of v0, /device:TPU:1, one launch (start us, length us, event | category | flops | bytes accessed | tf_op | source)
XLA Modules:
  0.0 569.8 jit_solution(3799169834706363901)
XLA Ops:
  12.9 12.3 %convolution_bitcast_fusion = f32[512,512]{0,1:T(8,128)} fusion(f32[10,256,512]{2,1,0:T(8,128)} %param.12), kind=kOutput, calls=%fused_computation.14 | convolution fusion | flops 8053063680 | bytes 6291456 | tf_op jit(solution)/shard_map/dot_general | solution.py:79
  26.5 96.5 %all_gather.12 = bf16[10,2048]{1,0:T(8,128)(2,1)S(1)} all-gather(bf16[10,256]{1,0:T(8,128)(2,1)S(1)} %convert_element_type.27), channel_id=1, replica_groups=mesh['samp'=16,'feat'=8] {'feat'}, dimensions={1}, use_global_device_ids=true | all-gather | bytes 46080 | tf_op jit(solution)/shard_map/all_gather | solution.py:75
  126.0 11.7 %cholesky.104 = f32[128,128]{1,0:T(8,128)S(1)} custom-call(f32[128,128]{1,0:T(8,128)S(1)} %cholesky.266), custom_call_target="Cholesky" | custom-call | tf_op jit(solution)/shard_map/jit(cholesky)/cholesky | solution.py:83
  137.9 9.8 %custom-call.33 = f32[1,128,128]{1,2,0:T(8,128)S(1)} custom-call(f32[1,128,128]{2,1,0:T(8,128)S(1)} %get-tuple-element.78), custom_call_target="InvertDiagBlocksLowerTriangular" | custom-call | tf_op jit(solution)/shard_map/jit(cholesky)/cholesky | solution.py:83
  148.4 11.7 %cholesky.217 = f32[128,128]{1,0:T(8,128)S(1)} custom-call(f32[128,128]{1,0:T(8,128)S(1)} %cholesky.270), custom_call_target="Cholesky" | custom-call | tf_op jit(solution)/shard_map/jit(cholesky)/cholesky | solution.py:83
  160.1 10.0 %custom-call.34 = f32[1,128,128]{1,2,0:T(8,128)S(1)} custom-call(f32[1,128,128]{2,1,0:T(8,128)S(1)} %get-tuple-element.75), custom_call_target="InvertDiagBlocksLowerTriangular" | custom-call | tf_op jit(solution)/shard_map/jit(cholesky)/cholesky | solution.py:83
  170.8 11.7 %cholesky.238 = f32[128,128]{1,0:T(8,128)S(1)} custom-call(f32[128,128]{1,0:T(8,128)S(1)} %cholesky.275), custom_call_target="Cholesky" | custom-call | tf_op jit(solution)/shard_map/jit(cholesky)/cholesky | solution.py:83
  182.5 9.8 %custom-call.35 = f32[1,128,128]{1,2,0:T(8,128)S(1)} custom-call(f32[1,128,128]{2,1,0:T(8,128)S(1)} %get-tuple-element.72), custom_call_target="InvertDiagBlocksLowerTriangular" | custom-call | tf_op jit(solution)/shard_map/jit(cholesky)/cholesky | solution.py:83
  192.9 11.9 %cholesky.255 = f32[128,128]{1,0:T(8,128)S(1)} custom-call(f32[128,128]{1,0:T(8,128)S(1)} %convolution_subtract_fusion.2), custom_call_target="Cholesky" | custom-call | tf_op jit(solution)/shard_map/jit(cholesky)/cholesky | solution.py:83
  208.2 11.6 %copy.14 = bf16[2048,8,256]{0,2,1:T(8,128)(2,1)} copy(bf16[2048,8,256]{2,0,1:T(8,128)(2,1)} %bitcast.1) | data formatting | bytes 16777216 | tf_op jit(solution)/shard_map/all_to_all | solution.py:54
  238.1 7.7 %all-to-all-start.2 = ((f32[16,10,256]{2,1,0:T(8,128)}), f32[16,10,256]{2,1,0:T(8,128)S(1)}, u32[]{:S(2)}, u32[]{:S(2)}) async-start(f32[16,10,256]{2,1,0:T(8,128)} %broadcast_in_dim.30), calls=%async_computation.2 | async-start | bytes 524288 | tf_op jit(solution)/shard_map/all_to_all | solution.py:16
  246.0 7.4 %all-to-all-done.2 = f32[16,10,256]{2,1,0:T(8,128)S(1)} async-done(((f32[16,10,256]{2,1,0:T(8,128)}), f32[16,10,256]{2,1,0:T(8,128)S(1)}, u32[]{:S(2)}, u32[]{:S(2)}) %all-to-all-start.2) | async-done | bytes 163872 | tf_op jit(solution)/shard_map/all_to_all | solution.py:16
  265.1 10.0 %while.12 = (s32[]{:T(128)}, f32[512,512]{1,0:T(8,128)S(1)}, s32[4,2]{0,1:T(2,128)S(1)}, f32[4,128,128]{2,1,0:T(8,128)}, s32[]{:T(128)}) while((s32[]{:T(128)}, f32[512,512]{1,0:T(8,128)S(1)}, s32[4,2]{0,1:T(2,128)S(1)}, f32[4,128,128]{2,1,0:T(8,128)}, s32[]{:T(128)}) %tuple.53), condition=%wide.while_cond.1, body=%wide.while_body.1.sunk | while | flops 2 | bytes 132205 | solution.py:92
  275.1 40.1 %custom-call.41 = f32[4,128,128]{1,2,0:T(8,128)S(1)} custom-call(f32[4,128,128]{2,1,0:T(8,128)} %get-tuple-element.48), custom_call_target="InvertDiagBlocksLowerTriangular" | custom-call | tf_op jit(solution)/shard_map/jit(_solve_triangular)/triangular_solve | solution.py:92
  318.3 6.8 %fusion.112 = f32[1,10,256]{2,0,1:T(1,128)S(1)} fusion(f32[10,256,512]{2,1,0:T(8,128)} %param.12, f32[128,1]{0,1:T(1,128)S(1)} %convolution_bitcast_fusion.30, f32[128,1]{0,1:T(1,128)S(1)} %convolution_bitcast_fusion.28, f32[128,1]{0,1:T(1,128)S(1)} %convolution_bitcast_fusion.26, f32[128,1]{0,1:T(1,128)S(1)} %convolution_bitcast_fusion.25), kind=kOutput, calls=%fused_computation.191 | convolution fusion | flops 15730176 | bytes 5255168 | tf_op jit(solution)/shard_map/dot_general | solution.py:95
  325.1 13.6 %all_gather.13 = bf16[10,2048]{1,0:T(8,128)(2,1)S(1)} all-gather(bf16[10,256]{1,0:T(8,128)(2,1)S(1)} %fusion.208), channel_id=1, replica_groups=mesh['samp'=16,'feat'=8] {'feat'}, dimensions={1}, use_global_device_ids=true | all-gather | bytes 46080 | tf_op jit(solution)/shard_map/all_gather | solution.py:107
  345.8 8.8 %all_to_all.113 = f32[8,10,256]{2,1,0:T(8,128)S(1)} all-to-all(f32[8,10,256]{2,1,0:T(8,128)S(1)} %fusion.11), channel_id=1, replica_groups=mesh['samp'=16,'feat'=8] {'feat'}, dimensions={0} | all-to-all | bytes 163840 | tf_op jit(solution)/shard_map/all_to_all | solution.py:33
  354.7 10.2 %all_to_all.114 = f32[16,10,256]{2,1,0:T(8,128)S(1)} all-to-all(f32[16,10,256]{2,1,0:T(8,128)S(1)} %broadcast_in_dim.33), channel_id=1, replica_groups=mesh['samp'=16,'feat'=8] {'samp'}, dimensions={0} | all-to-all | bytes 327680 | tf_op jit(solution)/shard_map/all_to_all | solution.py:16
  366.2 9.2 %all_to_all.115 = f32[8,1,1]{2,1,0:T(1,128)S(1)} all-to-all(f32[8,1,1]{2,1,0:T(1,128)S(1)} %broadcast_in_dim.32), channel_id=1, replica_groups=mesh['samp'=16,'feat'=8] {'feat'}, dimensions={0} | all-to-all | bytes 64 | tf_op jit(solution)/shard_map/all_to_all | solution.py:16
  392.1 7.7 %all_to_all.116 = f32[8,1,512]{2,1,0:T(1,128)S(1)} all-to-all(f32[8,1,512]{2,1,0:T(1,128)S(1)} %broadcast_in_dim.35), channel_id=1, replica_groups=mesh['samp'=16,'feat'=8] {'feat'}, dimensions={0} | all-to-all | bytes 32768 | tf_op jit(solution)/shard_map/all_to_all | solution.py:16
  402.8 6.8 %fusion.119 = f32[1,10,256]{2,0,1:T(1,128)S(1)} fusion(f32[10,256,512]{2,1,0:T(8,128)} %param.12, f32[128,1]{0,1:T(1,128)S(1)} %convolution_bitcast_fusion.18, f32[128,1]{0,1:T(1,128)S(1)} %convolution_bitcast_fusion.16, f32[128,1]{0,1:T(1,128)S(1)} %convolution_bitcast_fusion.14, f32[128,1]{0,1:T(1,128)S(1)} %convolution_bitcast_fusion.13), kind=kOutput, calls=%fused_computation.200 | convolution fusion | flops 15730176 | bytes 5255168 | tf_op jit(solution)/shard_map/dot_general | solution.py:95
  410.9 7.7 %all_to_all.117 = f32[8,1,1]{2,1,0:T(1,128)S(1)} all-to-all(f32[8,1,1]{2,1,0:T(1,128)S(1)} %broadcast_in_dim.36), channel_id=1, replica_groups=mesh['samp'=16,'feat'=8] {'feat'}, dimensions={0} | all-to-all | bytes 64 | tf_op jit(solution)/shard_map/all_to_all | solution.py:16
  420.5 13.3 %all_gather.14 = bf16[10,2048]{1,0:T(8,128)(2,1)S(1)} all-gather(bf16[10,256]{1,0:T(8,128)(2,1)S(1)} %get-tuple-element.65), channel_id=1, replica_groups=mesh['samp'=16,'feat'=8] {'feat'}, dimensions={1}, use_global_device_ids=true | all-gather | bytes 46080 | tf_op jit(solution)/shard_map/all_gather | solution.py:107
  444.0 7.9 %all_to_all.118 = f32[8,10,256]{2,1,0:T(8,128)S(1)} all-to-all(f32[8,10,256]{2,1,0:T(8,128)S(1)} %fusion.14), channel_id=1, replica_groups=mesh['samp'=16,'feat'=8] {'feat'}, dimensions={0} | all-to-all | bytes 163840 | tf_op jit(solution)/shard_map/all_to_all | solution.py:33
  452.0 10.2 %all_to_all.119 = f32[16,10,256]{2,1,0:T(8,128)S(1)} all-to-all(f32[16,10,256]{2,1,0:T(8,128)S(1)} %broadcast_in_dim.37), channel_id=1, replica_groups=mesh['samp'=16,'feat'=8] {'samp'}, dimensions={0} | all-to-all | bytes 327680 | tf_op jit(solution)/shard_map/all_to_all | solution.py:16
  463.4 9.4 %all_to_all.120 = f32[8,1,1]{2,1,0:T(1,128)S(1)} all-to-all(f32[8,1,1]{2,1,0:T(1,128)S(1)} %broadcast_in_dim.38), channel_id=1, replica_groups=mesh['samp'=16,'feat'=8] {'feat'}, dimensions={0} | all-to-all | bytes 64 | tf_op jit(solution)/shard_map/all_to_all | solution.py:16
  479.8 7.7 %all_to_all.121 = f32[8,1,512]{2,1,0:T(1,128)S(1)} all-to-all(f32[8,1,512]{2,1,0:T(1,128)S(1)} %broadcast_in_dim.39), channel_id=1, replica_groups=mesh['samp'=16,'feat'=8] {'feat'}, dimensions={0} | all-to-all | bytes 32768 | tf_op jit(solution)/shard_map/all_to_all | solution.py:16
  498.4 7.7 %all_to_all.122 = f32[8,1,1]{2,1,0:T(1,128)S(1)} all-to-all(f32[8,1,1]{2,1,0:T(1,128)S(1)} %broadcast_in_dim.40), channel_id=1, replica_groups=mesh['samp'=16,'feat'=8] {'feat'}, dimensions={0} | all-to-all | bytes 64 | tf_op jit(solution)/shard_map/all_to_all | solution.py:16
  508.0 13.3 %all_gather.15 = bf16[10,2048]{1,0:T(8,128)(2,1)S(1)} all-gather(bf16[10,256]{1,0:T(8,128)(2,1)S(1)} %get-tuple-element.63), channel_id=1, replica_groups=mesh['samp'=16,'feat'=8] {'feat'}, dimensions={1}, use_global_device_ids=true | all-gather | bytes 46080 | tf_op jit(solution)/shard_map/all_gather | solution.py:107
  531.5 7.9 %all_to_all.123 = f32[8,10,256]{2,1,0:T(8,128)S(1)} all-to-all(f32[8,10,256]{2,1,0:T(8,128)S(1)} %fusion.17), channel_id=1, replica_groups=mesh['samp'=16,'feat'=8] {'feat'}, dimensions={0} | all-to-all | bytes 163840 | tf_op jit(solution)/shard_map/all_to_all | solution.py:33
  539.5 10.2 %all_to_all.124 = f32[16,10,256]{2,1,0:T(8,128)S(1)} all-to-all(f32[16,10,256]{2,1,0:T(8,128)S(1)} %broadcast_in_dim.41), channel_id=1, replica_groups=mesh['samp'=16,'feat'=8] {'samp'}, dimensions={0} | all-to-all | bytes 327680 | tf_op jit(solution)/shard_map/all_to_all | solution.py:16
  551.0 9.2 %all_to_all.125 = f32[8,1,1]{2,1,0:T(1,128)S(1)} all-to-all(f32[8,1,1]{2,1,0:T(1,128)S(1)} %broadcast_in_dim.42), channel_id=1, replica_groups=mesh['samp'=16,'feat'=8] {'feat'}, dimensions={0} | all-to-all | bytes 64 | tf_op jit(solution)/shard_map/all_to_all | solution.py:16
  (167 shorter events, 126.0 us)
Async XLA Ops:
  6.5 201.7 %all-to-all-start = ((bf16[8,2048,256]{2,1,0:T(8,128)(2,1)}), bf16[8,2048,256]{2,1,0:T(8,128)(2,1)}, u32[]{:S(2)}, u32[]{:S(2)}) async-start(bf16[8,2048,256]{2,1,0:T(8,128)(2,1)} %bitcast.495), calls=%async_computation | async-start | bytes 16777216 | tf_op jit(solution)/shard_map/all_to_all | solution.py:54
  12.8 12.4 %copy-start = (f32[10,256]{1,0:T(8,128)S(1)}, f32[10,256]{1,0:T(8,128)}, u32[]{:S(2)}) copy-start(f32[10,256]{1,0:T(8,128)} %param.11) | copy-start | bytes 30724
  12.8 12.4 %copy-start.1 = (f32[512]{0:T(512)S(1)}, f32[512]{0:T(512)}, u32[]{:S(2)}) copy-start(f32[512]{0:T(512)} %param.13) | copy-start | bytes 6148
  12.8 110.2 %all-reduce.3.cloned.1.call-start = ((), (), s32[]{:S(2)}) async-start(), calls=%async_computation.18 | async-start | bytes 2097152 | tf_op jit(solution)/shard_map/psum | solution.py:82
  219.8 4.8 slice-start
  219.8 4.8 dynamic-slice-start
  219.8 5.9 %slice-start.1 = ((s8[8388608]{0:T(1024)(128)(4,1)}), s8[4194304]{0:T(1024)(128)(4,1)S(1)}, s32[]{:S(2)}) async-start(s8[8388608]{0:T(1024)(128)(4,1)} %bitcast.491), calls=%async_computation.20 | async-start | bytes 8388608
  228.6 8.7 %all-to-all-start.1 = ((f32[8,10,256]{2,1,0:T(8,128)}), f32[8,10,256]{2,1,0:T(8,128)S(1)}, u32[]{:S(2)}, u32[]{:S(2)}) async-start(f32[8,10,256]{2,1,0:T(8,128)} %fusion.8), calls=%async_computation.1 | async-start | bytes 262144 | tf_op jit(solution)/shard_map/all_to_all | solution.py:33
  238.1 15.3 %all-to-all-start.2 = ((f32[16,10,256]{2,1,0:T(8,128)}), f32[16,10,256]{2,1,0:T(8,128)S(1)}, u32[]{:S(2)}, u32[]{:S(2)}) async-start(f32[16,10,256]{2,1,0:T(8,128)} %broadcast_in_dim.30), calls=%async_computation.2 | async-start | bytes 524288 | tf_op jit(solution)/shard_map/all_to_all | solution.py:16
  259.2 56.1 %all-to-all-start.3 = ((f32[8,1,512]{2,1,0:T(1,128)}), f32[8,1,512]{2,1,0:T(1,128)S(1)}, u32[]{:S(2)}, u32[]{:S(2)}) async-start(f32[8,1,512]{2,1,0:T(1,128)} %broadcast_in_dim.31), calls=%async_computation.3 | async-start | bytes 32768 | tf_op jit(solution)/shard_map/all_to_all | solution.py:16
  325.1 18.4 %slice-start.2 = ((s8[8388608]{0:T(1024)(128)(4,1)}), s8[4194304]{0:T(1024)(128)(4,1)S(1)}, s32[]{:S(2)}) async-start(s8[8388608]{0:T(1024)(128)(4,1)} %bitcast.493), calls=%async_computation.21 | async-start | bytes 8388608
  338.7 4.8 slice-start.3
  376.5 8.6 %all-to-all-start.7 = ((f32[8,1,1]{2,1,0:T(1,128)}), f32[8,1,1]{2,1,0:T(1,128)S(1)}, u32[]{:S(2)}, u32[]{:S(2)}) async-start(f32[8,1,1]{2,1,0:T(1,128)} %broadcast_in_dim.34), calls=%async_computation.7 | async-start | bytes 8192 | tf_op jit(solution)/shard_map/all_to_all | solution.py:16
Sparse Core Ops, SparseCore 0:
  25.3 71.9 all-reduce.2
where the time goes:
time: 576 us; the launch traced here: 570 us
  blocking collectives  251 us (44%)
  other arithmetic  129 us (22%)
  matrix products  93.6 us (16%)
  local copies, waits for them, and re-layouts  30.1 us (5%)
  starting transfers between devices  27.6 us (5%)
  between operations  23.7 us (4%)
  waiting for transfers between devices  15.4 us (3%)
    all_gather x1, blocking collectives, on_device(): weights_b = lax.all_gather(weights_b, 'feat', axis=1, tiled=True)  96.5 us
    all_to_all x10, blocking collectives, copy_for_each(): lax.all_to_all(jnp.broadcast_to(shard[None], (devices, *shard.shape)), ax...  89.2 us
    another operation x14, other arithmetic, on_device(): factor = jnp.linalg.cholesky(gram_matrix)  78.8 us
    another operation x4, other arithmetic, precondition(): jax.scipy.linalg.solve_triangular(factor, weighted_coords, lower=True, tr...  40.3 us
    all_gather x3, blocking collectives, on_device(): gathered = lax.all_gather(gathered, 'feat', axis=1, tiled=True)  40.2 us
    all_to_all x3, blocking collectives, summed_on_arrival(): lax.all_to_all(in_blocks(shard, dim, devices), axis, 0, 0, tiled=True)  24.7 us
    dot_general x3, matrix products, precondition(): jnp.dot(basis_own, outer_coords, precision=lax.Precision.HIGHEST)  20.5 us
    dot_general x4, matrix products, class_logits(): lax.dot_general(rounded, row_features, contract_last, preferred_element_t...  18.7 us
  transfers between devices with their start and end apart: 6, of which 3 were waited for; matrix products, arithmetic and copies ran while one was open for 26% of the time, Pallas kernels for 0%

commit v1 on v0

--- a/solution.py
+++ b/solution.py
@@ -72,7 +72,9 @@
         return of_everyone(partial_cols, "samp")
 
     weights_b = weights.astype(jnp.bfloat16)
-    weights_b = lax.all_gather(weights_b, "feat", axis=1, tiled=True)
+    weights_b = jnp.concatenate(
+        lax.all_to_all(jnp.stack([weights_b] * lax.axis_size("feat")), "feat", 0, 0), axis=1
+    )
     probabilities = column_softmax(class_logits(weights_b) / math.sqrt(F))
     gradient = feature_sums(probabilities - onehot) * (math.sqrt(F) / total_rows) + ridge * weights
     flat_local = sketch_basis.reshape(classes * local_cols, sketch_rank)

time: 576 us -> 577 us (level)
  blocking collectives: 251 us -> 154 us
  waiting for transfers between devices: 15.4 us -> 86.2 us
  starting transfers between devices: 27.6 us -> 52.5 us
    all_gather x1 -> x0, blocking collectives: 96.5 us -> none  [on_device(): weights_b = lax.all_gather(weights_b, 'feat', axis=1, tiled=True)]
    psum x1, waiting for transfers between devices: 0.01 us -> 70.8 us  [on_device(): gram_matrix = lax.psum(local_gram, 'feat')]
    all_to_all x0 -> x1, starting transfers between devices: none -> 23.9 us  [on_device(): lax.all_to_all(jnp.stack([weights_b] * lax.axis_size('feat')), 'feat', 0, 0)]
  transfers between devices with their start and end apart: 6 -> 7, of which waited for: 3 -> 4; matrix products, arithmetic and copies ran while one was open for 26% -> 28% of each run, Pallas kernels for 0% -> 0%
where the time goes in v1:
time: 577 us; the launch traced here: 571 us
  blocking collectives  154 us (27%)
  other arithmetic  129 us (22%)
  matrix products  94.9 us (16%)
  waiting for transfers between devices  86.2 us (15%)
  starting transfers between devices  52.5 us (9%)
  local copies, waits for them, and re-layouts  30.1 us (5%)
  between operations  23.9 us (4%)
    all_to_all x10, blocking collectives, copy_for_each(): lax.all_to_all(jnp.broadcast_to(shard[None], (devices, *shard.shape)), ax...  89.3 us
    another operation x14, other arithmetic, on_device(): factor = jnp.linalg.cholesky(gram_matrix)  78.9 us
    psum x1, waiting for transfers between devices, on_device(): gram_matrix = lax.psum(local_gram, 'feat')  70.8 us
    another operation x4, other arithmetic, precondition(): jax.scipy.linalg.solve_triangular(factor, weighted_coords, lower=True, tr...  40.3 us
    all_gather x3, blocking collectives, on_device(): gathered = lax.all_gather(gathered, 'feat', axis=1, tiled=True)  40.2 us
    all_to_all x3, blocking collectives, summed_on_arrival(): lax.all_to_all(in_blocks(shard, dim, devices), axis, 0, 0, tiled=True)  24.7 us
    all_to_all x1, starting transfers between devices, on_device(): lax.all_to_all(jnp.stack([weights_b] * lax.axis_size('feat')), 'feat', 0, 0)  23.9 us
    dot_general x3, matrix products, precondition(): jnp.dot(basis_own, outer_coords, precision=lax.Precision.HIGHEST)  20.5 us
  transfers between devices with their start and end apart: 7, of which 4 were waited for; matrix products, arithmetic and copies ran while one was open for 28% of the time, Pallas kernels for 0%

profile of v1, /device:TPU:1, one launch (start us, length us, event | category | flops | bytes accessed | tf_op | source)
XLA Modules:
  0.0 570.6 jit_solution(13249832406405929882)
XLA Ops:
  12.9 12.5 %convolution_bitcast_fusion.1 = f32[512,512]{0,1:T(8,128)} fusion(f32[10,256,512]{2,1,0:T(8,128)} %param.12), kind=kOutput, calls=%fused_computation.15 | convolution fusion | flops 8053063680 | bytes 6291456 | tf_op jit(solution)/shard_map/dot_general | solution.py:81
  26.7 70.8 %all-reduce.3.cloned.1.call-done = f32[512,512]{0,1:T(8,128)} async-done(((f32[512,512]{0,1:T(8,128)}), f32[512,512]{0,1:T(8,128)}) %all-reduce.3.cloned.1.call-update) | async-done | bytes 1048592 | tf_op jit(solution)/shard_map/psum | solution.py:84
  100.5 11.7 %cholesky.104 = f32[128,128]{1,0:T(8,128)S(1)} custom-call(f32[128,128]{1,0:T(8,128)S(1)} %cholesky.266), custom_call_target="Cholesky" | custom-call | tf_op jit(solution)/shard_map/jit(cholesky)/cholesky | solution.py:85
  112.4 9.8 %custom-call.33 = f32[1,128,128]{1,2,0:T(8,128)S(1)} custom-call(f32[1,128,128]{2,1,0:T(8,128)S(1)} %get-tuple-element.78), custom_call_target="InvertDiagBlocksLowerTriangular" | custom-call | tf_op jit(solution)/shard_map/jit(cholesky)/cholesky | solution.py:85
  122.9 11.7 %cholesky.217 = f32[128,128]{1,0:T(8,128)S(1)} custom-call(f32[128,128]{1,0:T(8,128)S(1)} %cholesky.270), custom_call_target="Cholesky" | custom-call | tf_op jit(solution)/shard_map/jit(cholesky)/cholesky | solution.py:85
  134.7 10.3 %custom-call.34 = f32[1,128,128]{1,2,0:T(8,128)S(1)} custom-call(f32[1,128,128]{2,1,0:T(8,128)S(1)} %get-tuple-element.75), custom_call_target="InvertDiagBlocksLowerTriangular" | custom-call | tf_op jit(solution)/shard_map/jit(cholesky)/cholesky | solution.py:85
  145.6 11.7 %cholesky.238 = f32[128,128]{1,0:T(8,128)S(1)} custom-call(f32[128,128]{1,0:T(8,128)S(1)} %cholesky.275), custom_call_target="Cholesky" | custom-call | tf_op jit(solution)/shard_map/jit(cholesky)/cholesky | solution.py:85
  157.3 9.8 %custom-call.35 = f32[1,128,128]{1,2,0:T(8,128)S(1)} custom-call(f32[1,128,128]{2,1,0:T(8,128)S(1)} %get-tuple-element.72), custom_call_target="InvertDiagBlocksLowerTriangular" | custom-call | tf_op jit(solution)/shard_map/jit(cholesky)/cholesky | solution.py:85
  167.8 11.7 %cholesky.255 = f32[128,128]{1,0:T(8,128)S(1)} custom-call(f32[128,128]{1,0:T(8,128)S(1)} %convolution_subtract_fusion.2), custom_call_target="Cholesky" | custom-call | tf_op jit(solution)/shard_map/jit(cholesky)/cholesky | solution.py:85
  180.9 23.9 %all-to-all-start = ((bf16[8,10,256]{2,1,0:T(8,128)(2,1)}), bf16[8,10,256]{2,1,0:T(8,128)(2,1)S(1)}, u32[]{:S(2)}, u32[]{:S(2)}) async-start(bf16[8,10,256]{2,1,0:T(8,128)(2,1)} %stack.2), calls=%async_computation | async-start | bytes 131072 | tf_op jit(solution)/shard_map/all_to_all | solution.py:76
  207.3 11.6 %copy.17 = bf16[2048,8,256]{0,2,1:T(8,128)(2,1)} copy(bf16[2048,8,256]{2,0,1:T(8,128)(2,1)} %bitcast.2) | data formatting | bytes 16777216 | tf_op jit(solution)/shard_map/all_to_all | solution.py:54
  238.6 7.6 %all-to-all-start.3 = ((f32[16,10,256]{2,1,0:T(8,128)}), f32[16,10,256]{2,1,0:T(8,128)S(1)}, u32[]{:S(2)}, u32[]{:S(2)}) async-start(f32[16,10,256]{2,1,0:T(8,128)} %broadcast_in_dim.30), calls=%async_computation.3 | async-start | bytes 524288 | tf_op jit(solution)/shard_map/all_to_all | solution.py:16
  246.3 7.4 %all-to-all-done.3 = f32[16,10,256]{2,1,0:T(8,128)S(1)} async-done(((f32[16,10,256]{2,1,0:T(8,128)}), f32[16,10,256]{2,1,0:T(8,128)S(1)}, u32[]{:S(2)}, u32[]{:S(2)}) %all-to-all-start.3) | async-done | bytes 163872 | tf_op jit(solution)/shard_map/all_to_all | solution.py:16
  265.2 10.5 %while.12 = (s32[]{:T(128)}, f32[512,512]{1,0:T(8,128)S(1)}, s32[4,2]{0,1:T(2,128)S(1)}, f32[4,128,128]{2,1,0:T(8,128)}, s32[]{:T(128)}) while((s32[]{:T(128)}, f32[512,512]{1,0:T(8,128)S(1)}, s32[4,2]{0,1:T(2,128)S(1)}, f32[4,128,128]{2,1,0:T(8,128)}, s32[]{:T(128)}) %tuple.53), condition=%wide.while_cond.1, body=%wide.while_body.1.sunk | while | flops 2 | bytes 132205 | solution.py:94
  275.6 40.1 %custom-call.41 = f32[4,128,128]{1,2,0:T(8,128)S(1)} custom-call(f32[4,128,128]{2,1,0:T(8,128)} %get-tuple-element.48), custom_call_target="InvertDiagBlocksLowerTriangular" | custom-call | tf_op jit(solution)/shard_map/jit(_solve_triangular)/triangular_solve | solution.py:94
  325.6 13.6 %all_gather.9 = bf16[10,2048]{1,0:T(8,128)(2,1)S(1)} all-gather(bf16[10,256]{1,0:T(8,128)(2,1)S(1)} %fusion.211), channel_id=1, replica_groups=mesh['samp'=16,'feat'=8] {'feat'}, dimensions={1}, use_global_device_ids=true | all-gather | bytes 46080 | tf_op jit(solution)/shard_map/all_gather | solution.py:109
  346.3 8.8 %all_to_all.118 = f32[8,10,256]{2,1,0:T(8,128)S(1)} all-to-all(f32[8,10,256]{2,1,0:T(8,128)S(1)} %fusion.12), channel_id=1, replica_groups=mesh['samp'=16,'feat'=8] {'feat'}, dimensions={0} | all-to-all | bytes 163840 | tf_op jit(solution)/shard_map/all_to_all | solution.py:33
  355.2 10.2 %all_to_all.119 = f32[16,10,256]{2,1,0:T(8,128)S(1)} all-to-all(f32[16,10,256]{2,1,0:T(8,128)S(1)} %broadcast_in_dim.33), channel_id=1, replica_groups=mesh['samp'=16,'feat'=8] {'samp'}, dimensions={0} | all-to-all | bytes 327680 | tf_op jit(solution)/shard_map/all_to_all | solution.py:16
  366.7 9.2 %all_to_all.120 = f32[8,1,1]{2,1,0:T(1,128)S(1)} all-to-all(f32[8,1,1]{2,1,0:T(1,128)S(1)} %broadcast_in_dim.32), channel_id=1, replica_groups=mesh['samp'=16,'feat'=8] {'feat'}, dimensions={0} | all-to-all | bytes 64 | tf_op jit(solution)/shard_map/all_to_all | solution.py:16
  392.7 7.7 %all_to_all.121 = f32[8,1,512]{2,1,0:T(1,128)S(1)} all-to-all(f32[8,1,512]{2,1,0:T(1,128)S(1)} %broadcast_in_dim.35), channel_id=1, replica_groups=mesh['samp'=16,'feat'=8] {'feat'}, dimensions={0} | all-to-all | bytes 32768 | tf_op jit(solution)/shard_map/all_to_all | solution.py:16
  403.4 6.8 %fusion.121 = f32[1,10,256]{2,0,1:T(1,128)S(1)} fusion(f32[10,256,512]{2,1,0:T(8,128)} %param.12, f32[128,1]{0,1:T(1,128)S(1)} %convolution_bitcast_fusion.19, f32[128,1]{0,1:T(1,128)S(1)} %convolution_bitcast_fusion.17, f32[128,1]{0,1:T(1,128)S(1)} %convolution_bitcast_fusion.15, f32[128,1]{0,1:T(1,128)S(1)} %convolution_bitcast_fusion.14), kind=kOutput, calls=%fused_computation.202 | convolution fusion | flops 15730176 | bytes 5255168 | tf_op jit(solution)/shard_map/dot_general | solution.py:97
  411.5 7.7 %all_to_all.122 = f32[8,1,1]{2,1,0:T(1,128)S(1)} all-to-all(f32[8,1,1]{2,1,0:T(1,128)S(1)} %broadcast_in_dim.36), channel_id=1, replica_groups=mesh['samp'=16,'feat'=8] {'feat'}, dimensions={0} | all-to-all | bytes 64 | tf_op jit(solution)/shard_map/all_to_all | solution.py:16
  421.0 13.3 %all_gather.10 = bf16[10,2048]{1,0:T(8,128)(2,1)S(1)} all-gather(bf16[10,256]{1,0:T(8,128)(2,1)S(1)} %get-tuple-element.65), channel_id=1, replica_groups=mesh['samp'=16,'feat'=8] {'feat'}, dimensions={1}, use_global_device_ids=true | all-gather | bytes 46080 | tf_op jit(solution)/shard_map/all_gather | solution.py:109
  444.6 7.9 %all_to_all.123 = f32[8,10,256]{2,1,0:T(8,128)S(1)} all-to-all(f32[8,10,256]{2,1,0:T(8,128)S(1)} %fusion.15), channel_id=1, replica_groups=mesh['samp'=16,'feat'=8] {'feat'}, dimensions={0} | all-to-all | bytes 163840 | tf_op jit(solution)/shard_map/all_to_all | solution.py:33
  452.6 10.2 %all_to_all.124 = f32[16,10,256]{2,1,0:T(8,128)S(1)} all-to-all(f32[16,10,256]{2,1,0:T(8,128)S(1)} %broadcast_in_dim.37), channel_id=1, replica_groups=mesh['samp'=16,'feat'=8] {'samp'}, dimensions={0} | all-to-all | bytes 327680 | tf_op jit(solution)/shard_map/all_to_all | solution.py:16
  463.9 9.5 %all_to_all.125 = f32[8,1,1]{2,1,0:T(1,128)S(1)} all-to-all(f32[8,1,1]{2,1,0:T(1,128)S(1)} %broadcast_in_dim.38), channel_id=1, replica_groups=mesh['samp'=16,'feat'=8] {'feat'}, dimensions={0} | all-to-all | bytes 64 | tf_op jit(solution)/shard_map/all_to_all | solution.py:16
  480.3 7.7 %all_to_all.126 = f32[8,1,512]{2,1,0:T(1,128)S(1)} all-to-all(f32[8,1,512]{2,1,0:T(1,128)S(1)} %broadcast_in_dim.39), channel_id=1, replica_groups=mesh['samp'=16,'feat'=8] {'feat'}, dimensions={0} | all-to-all | bytes 32768 | tf_op jit(solution)/shard_map/all_to_all | solution.py:16
  499.0 7.7 %all_to_all.127 = f32[8,1,1]{2,1,0:T(1,128)S(1)} all-to-all(f32[8,1,1]{2,1,0:T(1,128)S(1)} %broadcast_in_dim.40), channel_id=1, replica_groups=mesh['samp'=16,'feat'=8] {'feat'}, dimensions={0} | all-to-all | bytes 64 | tf_op jit(solution)/shard_map/all_to_all | solution.py:16
  508.6 13.3 %all_gather.11 = bf16[10,2048]{1,0:T(8,128)(2,1)S(1)} all-gather(bf16[10,256]{1,0:T(8,128)(2,1)S(1)} %get-tuple-element.63), channel_id=1, replica_groups=mesh['samp'=16,'feat'=8] {'feat'}, dimensions={1}, use_global_device_ids=true | all-gather | bytes 46080 | tf_op jit(solution)/shard_map/all_gather | solution.py:109
  532.1 7.9 %all_to_all.128 = f32[8,10,256]{2,1,0:T(8,128)S(1)} all-to-all(f32[8,10,256]{2,1,0:T(8,128)S(1)} %fusion.18), channel_id=1, replica_groups=mesh['samp'=16,'feat'=8] {'feat'}, dimensions={0} | all-to-all | bytes 163840 | tf_op jit(solution)/shard_map/all_to_all | solution.py:33
  540.1 10.2 %all_to_all.129 = f32[16,10,256]{2,1,0:T(8,128)S(1)} all-to-all(f32[16,10,256]{2,1,0:T(8,128)S(1)} %broadcast_in_dim.41), channel_id=1, replica_groups=mesh['samp'=16,'feat'=8] {'samp'}, dimensions={0} | all-to-all | bytes 327680 | tf_op jit(solution)/shard_map/all_to_all | solution.py:16
  551.6 9.2 %all_to_all.130 = f32[8,1,1]{2,1,0:T(1,128)S(1)} all-to-all(f32[8,1,1]{2,1,0:T(1,128)S(1)} %broadcast_in_dim.42), channel_id=1, replica_groups=mesh['samp'=16,'feat'=8] {'feat'}, dimensions={0} | all-to-all | bytes 64 | tf_op jit(solution)/shard_map/all_to_all | solution.py:16
  (166 shorter events, 135.0 us)
Async XLA Ops:
  6.5 173.7 %all-to-all-start.1 = ((bf16[8,2048,256]{2,1,0:T(8,128)(2,1)}), bf16[8,2048,256]{2,1,0:T(8,128)(2,1)}, u32[]{:S(2)}, u32[]{:S(2)}) async-start(bf16[8,2048,256]{2,1,0:T(8,128)(2,1)} %bitcast.503), calls=%async_computation.1 | async-start | bytes 16777216 | tf_op jit(solution)/shard_map/all_to_all | solution.py:54
  12.8 12.6 %copy-start.1 = (f32[10,256]{1,0:T(8,128)S(1)}, f32[10,256]{1,0:T(8,128)}, u32[]{:S(2)}) copy-start(f32[10,256]{1,0:T(8,128)} %param.11) | copy-start | bytes 30724
  12.8 12.6 %copy-start.2 = (f32[512]{0:T(512)S(1)}, f32[512]{0:T(512)}, u32[]{:S(2)}) copy-start(f32[512]{0:T(512)} %param.13) | copy-start | bytes 6148
  12.8 84.7 %all-reduce.3.cloned.1.call-start = ((), (), s32[]{:S(2)}) async-start(), calls=%async_computation.19 | async-start | bytes 2097152 | tf_op jit(solution)/shard_map/psum | solution.py:84
  180.9 38.1 %all-to-all-start = ((bf16[8,10,256]{2,1,0:T(8,128)(2,1)}), bf16[8,10,256]{2,1,0:T(8,128)(2,1)S(1)}, u32[]{:S(2)}, u32[]{:S(2)}) async-start(bf16[8,10,256]{2,1,0:T(8,128)(2,1)} %stack.2), calls=%async_computation | async-start | bytes 131072 | tf_op jit(solution)/shard_map/all_to_all | solution.py:76
  218.9 5.9 %dynamic-slice-start = ((s32[16384]{0:T(1024)}, s32[]{:T(128)}), s32[2048]{0:T(1024)S(1)}, s32[]{:S(2)}) async-start(s32[16384]{0:T(1024)} %param.10, s32[]{:T(128)} %select_n.7), calls=%async_computation.22 | async-start | bytes 16896 | tf_op jit(solution)/shard_map/dynamic_slice | solution.py:57
  218.9 5.9 %copy-start = (bf16[2048,8,256]{0,2,1:T(8,128)(2,1)S(1)}, bf16[2048,8,256]{0,2,1:T(8,128)(2,1)}, u32[]{:S(2)}) copy-start(bf16[2048,8,256]{0,2,1:T(8,128)(2,1)} %copy.17) | copy-start | bytes 25165828
  227.8 10.1 %all-to-all-start.2 = ((f32[8,10,256]{2,1,0:T(8,128)}), f32[8,10,256]{2,1,0:T(8,128)S(1)}, u32[]{:S(2)}, u32[]{:S(2)}) async-start(f32[8,10,256]{2,1,0:T(8,128)} %fusion.9), calls=%async_computation.2 | async-start | bytes 262144 | tf_op jit(solution)/shard_map/all_to_all | solution.py:33
  238.6 15.2 %all-to-all-start.3 = ((f32[16,10,256]{2,1,0:T(8,128)}), f32[16,10,256]{2,1,0:T(8,128)S(1)}, u32[]{:S(2)}, u32[]{:S(2)}) async-start(f32[16,10,256]{2,1,0:T(8,128)} %broadcast_in_dim.30), calls=%async_computation.3 | async-start | bytes 524288 | tf_op jit(solution)/shard_map/all_to_all | solution.py:16
  259.4 56.3 %all-to-all-start.4 = ((f32[8,1,512]{2,1,0:T(1,128)}), f32[8,1,512]{2,1,0:T(1,128)S(1)}, u32[]{:S(2)}, u32[]{:S(2)}) async-start(f32[8,1,512]{2,1,0:T(1,128)} %broadcast_in_dim.31), calls=%async_computation.4 | async-start | bytes 32768 | tf_op jit(solution)/shard_map/all_to_all | solution.py:16
  325.6 18.4 %slice-start = ((s8[8388608]{0:T(1024)(128)(4,1)}), s8[4194304]{0:T(1024)(128)(4,1)S(1)}, s32[]{:S(2)}) async-start(s8[8388608]{0:T(1024)(128)(4,1)} %bitcast.501), calls=%async_computation.20 | async-start | bytes 8388608
  339.2 4.8 slice-start.1
  377.0 8.7 %all-to-all-start.8 = ((f32[8,1,1]{2,1,0:T(1,128)}), f32[8,1,1]{2,1,0:T(1,128)S(1)}, u32[]{:S(2)}, u32[]{:S(2)}) async-start(f32[8,1,1]{2,1,0:T(1,128)} %broadcast_in_dim.34), calls=%async_computation.8 | async-start | bytes 8192 | tf_op jit(solution)/shard_map/all_to_all | solution.py:16
Sparse Core Ops, SparseCore 0:
  25.5 71.9 all-reduce.2
